TPU v7x, 32 devices: a whole 2x2x4 slice. The times are simulated.
32 devices in a mesh: patch: 8 (over y, x, core), tensor: 4 (over z).
Axes of the slice: x: 2, y: 2, z: 4, core: 2. Of those that a mesh axis runs over, the one named last changes fastest.
Arguments:
- tokens: bfloat16 [8192, 3072], P(('patch', 'tensor')), may hold values from -6 to 6
- text_tokens: bfloat16 [512, 3072], P('patch'), may hold values from -6 to 6
- img_shift: float32 [3072], replicated, may hold values from -3 to 3
- img_scale: float32 [3072], replicated, may hold values from -3 to 3
- img_gate: float32 [3072], replicated, may hold values from 0.5 to 2
- txt_shift: float32 [3072], replicated, may hold values from -3 to 3
- txt_scale: float32 [3072], replicated, may hold values from -3 to 3
- qkv_weight: bfloat16 [3072, 3, 2048], P(None, None, 'tensor'), may hold values from -0.109375 to 0.109375
- txt_kv_weight: bfloat16 [3072, 2, 2048], P(None, None, 'tensor'), may hold values from -0.109375 to 0.109375
- q_gain: float32 [128], replicated, may hold values from 1 to 3
- k_gain: float32 [128], replicated, may hold values from 1 to 3
- txt_k_gain: float32 [128], replicated, may hold values from 1 to 3
- out_weight: bfloat16 [2048, 3072], P('tensor'), may hold values from -0.125 to 0.125
- stale_keys: bfloat16 [8192, 2048], P('patch', 'tensor'), may hold values from -600 to 600
- stale_values: bfloat16 [8192, 2048], P('patch', 'tensor'), may hold values from -6 to 6
Outputs:
- updated: bfloat16 [8192, 3072], P(('patch', 'tensor'))
- new_keys: bfloat16 [8192, 2048], P('patch', 'tensor')
- new_values: bfloat16 [8192, 2048], P('patch', 'tensor')
All inputs are finite; a program needn't handle non-finite values.
Results may differ from a plain program's by a relative error of at most 0.015.
The roundings to bfloat16 on the way count: a program that leaves them out, or rounds other values in their place, can miss the bound.
Values may be sent and summed in bfloat16 or wider, within the bound.
No kernel may reach another device: no remote copies, remote signals or barrier semaphores. Data moves between devices by JAX's collectives and lax.ppermute only.
A program may use at most 320 MiB of HBM per device.

v0:
```python
import jax
import jax.numpy as jnp
from jax import lax
from jax.sharding import PartitionSpec as P


def layer_mod(values, shift_vec, scale_vec):
    wide = values.astype(jnp.float32)
    centre = jnp.mean(wide, axis=-1, keepdims=True)
    spread = jnp.mean((wide - centre) * (wide - centre), axis=-1, keepdims=True)
    normed = (wide - centre) * lax.rsqrt(spread + 1e-06)
    return ((1.0 + scale_vec) * normed + shift_vec).astype(jnp.bfloat16)


def rms_gain(values, gain_vec):
    square = jnp.mean(values * values, axis=-1, keepdims=True)
    return values * lax.rsqrt(square + 1e-06) * gain_vec


def absorb(running, queries, key_rows, value_rows, keep_mask, factor):
    old_peak, denominator, numerator = running
    scores = (
        jnp.einsum("qhd,khd->hqk", queries, key_rows, preferred_element_type=jnp.float32) * factor
    )
    if keep_mask is not None:
        scores = jnp.where(keep_mask[None, None, :], scores, -1e30)
    new_peak = jnp.maximum(old_peak, jnp.max(scores, axis=-1))
    rescale = jnp.exp(old_peak - new_peak)
    weights = jnp.exp(scores - new_peak[:, :, None])
    denominator = denominator * rescale + jnp.sum(weights, axis=-1)
    numerator = numerator * jnp.transpose(rescale)[:, :, None] + jnp.einsum(
        "hqk,khd->qhd", weights.astype(jnp.bfloat16), value_rows, preferred_element_type=jnp.float32
    )
    return (new_peak, denominator, numerator)


def per_device(
    tokens,
    text_tokens,
    img_shift,
    img_scale,
    img_gate,
    txt_shift,
    txt_scale,
    qkv_weight,
    txt_kv_weight,
    q_gain,
    k_gain,
    txt_k_gain,
    out_weight,
    stale_keys,
    stale_values,
):
    width = tokens.shape[1]
    head_dim = q_gain.shape[0]
    local_heads = qkv_weight.shape[2] // head_dim
    factor = 1.0 / float(head_dim) ** 0.5
    image_mod = layer_mod(tokens, img_shift, img_scale)
    flat_weight = qkv_weight.reshape(width, 3 * local_heads * head_dim)
    projected = jnp.dot(
        lax.all_gather(image_mod, "tensor", axis=0, tiled=True),
        flat_weight,
        preferred_element_type=jnp.float32,
    )
    patch_rows = projected.shape[0]
    projected = projected.reshape(patch_rows, 3, local_heads, head_dim)
    queries = rms_gain(projected[:, 0], q_gain).astype(jnp.bfloat16)
    fresh_keys = rms_gain(projected[:, 1], k_gain).astype(jnp.bfloat16)
    fresh_values = projected[:, 2].astype(jnp.bfloat16)
    text_mod = layer_mod(text_tokens, txt_shift, txt_scale)
    text_proj = jnp.dot(
        text_mod,
        txt_kv_weight.reshape(width, 2 * local_heads * head_dim),
        preferred_element_type=jnp.float32,
    )
    text_proj = text_proj.reshape(text_mod.shape[0], 2, local_heads, head_dim)
    text_keys = rms_gain(text_proj[:, 0], txt_k_gain).astype(jnp.bfloat16)
    text_values = text_proj[:, 1].astype(jnp.bfloat16)
    text_pairs = jnp.stack([text_keys, text_values], axis=1)
    all_text = lax.all_gather(text_pairs, "patch", axis=0, tiled=True)
    running = (
        jnp.full((local_heads, patch_rows), -1e30, jnp.float32),
        jnp.zeros((local_heads, patch_rows), jnp.float32),
        jnp.zeros((patch_rows, local_heads, head_dim), jnp.float32),
    )
    first_keys = jnp.concatenate([fresh_keys, all_text[:, 0]], axis=0)
    first_values = jnp.concatenate([fresh_values, all_text[:, 1]], axis=0)
    running = absorb(running, queries, first_keys, first_values, None, factor)
    own_start = lax.axis_index("patch") * patch_rows
    key_rows = lax.all_gather(stale_keys, "patch", axis=0, tiled=True).reshape(
        -1, local_heads, head_dim
    )
    value_rows = lax.all_gather(stale_values, "patch", axis=0, tiled=True).reshape(
        -1, local_heads, head_dim
    )
    positions = jnp.arange(key_rows.shape[0], dtype=jnp.int32)
    keep_mask = (positions < own_start) | (positions >= own_start + patch_rows)
    running = absorb(running, queries, key_rows, value_rows, keep_mask, factor)
    denominator = running[1]
    numerator = running[2]
    attended = (numerator / jnp.transpose(denominator)[:, :, None]).astype(jnp.bfloat16)
    attended = attended.reshape(patch_rows, local_heads * head_dim)
    branch = lax.psum_scatter(
        jnp.dot(attended, out_weight, preferred_element_type=jnp.float32).astype(jnp.bfloat16),
        "tensor",
        scatter_dimension=0,
        tiled=True,
    ).astype(jnp.float32)
    updated = (tokens.astype(jnp.float32) + img_gate * branch).astype(jnp.bfloat16)
    return (
        updated,
        fresh_keys.reshape(patch_rows, local_heads * head_dim),
        fresh_values.reshape(patch_rows, local_heads * head_dim),
    )


def solution(mesh):
    placed = (
        P(("patch", "tensor"), None),
        P("patch", None),
        P(),
        P(),
        P(),
        P(),
        P(),
        P(None, None, "tensor"),
        P(None, None, "tensor"),
        P(),
        P(),
        P(),
        P("tensor", None),
        P("patch", "tensor"),
        P("patch", "tensor"),
    )
    return jax.shard_map(
        per_device,
        mesh=mesh,
        in_specs=placed,
        out_specs=(P(("patch", "tensor"), None), P("patch", "tensor"), P("patch", "tensor")),
        check_vma=False,
    )
```

profile of v0, /device:TPU:0, one launch (start us, length us, event | category | flops | bytes accessed | tf_op | source)
XLA Modules:
  0.0 531.7 jit_solution(4409786438920954687)
XLA Ops:
  7.2 0.0 copy-start
  7.2 0.0 all-gather.7.cloned.1.call-start
  7.2 7.6 %copy.63 = bf16[384,8,2,512]{3,1,2,0:T(8,128)(2,1)} copy(bf16[384,8,2,512]{3,2,1,0:T(2,128)(2,1)} %bitcast.102) | data formatting | bytes 12582912
  14.9 8.7 %copy.42 = bf16[1024,3072]{1,0:T(8,128)(2,1)} copy(bf16[1024,3072]{0,1:T(8,128)(2,1)} %bitcast.96) | data formatting | bytes 12582912 | tf_op jit(solution)/shard_map/dot_general | solution.py:71
  23.5 0.0 copy-done.3
  23.5 0.2 convert_reduce_fusion.1
  23.7 0.3 fusion.38
  24.0 0.0 copy-done.11
  24.0 0.0 copy-start.16
  24.0 4.8 fusion.43
  28.9 0.0 copy-start.12
  28.9 0.0 copy-start.10
  28.9 0.1 multiply_reduce_fusion.2
  29.0 0.1 multiply_convert_fusion.2
  29.2 0.8 copy.43
  29.9 0.0 all-gather.7.cloned.1.call-update
  30.0 0.0 all-gather.5.cloned.1.call-start
  30.0 0.0 copy-start.2
  30.0 1.8 convert_reduce_fusion
  31.8 2.0 fusion.16
  33.8 0.0 copy-done.12
  33.9 1.9 fusion.19
  35.8 0.0 all-gather.5.cloned.1.call-update
  35.8 0.0 all-gather.9.cloned.1.call-start
  35.9 2.3 copy.48
  38.1 0.0 all-gather.9.cloned.1.call-update
  38.2 0.0 all-gather.11.cloned.1.call-start
  38.2 0.5 all-gather.11.cloned.1.call-update
  38.7 0.2 reduce-scatter.2.cloned.1.call-start
  39.0 12.8 %copy.41 = bf16[3072,3,512]{0,2,1:T(8,128)(2,1)} copy(bf16[3072,3,512]{2,0,1:T(8,128)(2,1)} %param.22) | data formatting | bytes 18874368 | tf_op args[7]
  51.8 4.4 all-gather.7.cloned.1.call-done
  56.2 2.5 fusion.62
  58.7 2.1 copy.61
  60.8 2.1 copy.62
  63.0 110.8 %all-gather.5.cloned.1.call-done = bf16[1024,3072]{1,0:T(8,128)(2,1)} async-done(((bf16[256,3072]{1,0:T(8,128)(2,1)}), bf16[1024,3072]{1,0:T(8,128)(2,1)}) %all-gather.5.cloned.1.call-update) | async-done | bytes 6291472 | tf_op jit(solution)/shard_map/all_gather | solution.py:61
  173.7 14.4 %fusion.12 = f32[1024,3,4,128]{0,3,2,1:T(8,128)S(1)} fusion(bf16[3,4,128,3072]{3,2,1,0:T(8,128)(2,1)} %bitcast.97, bf16[1024,3072]{1,0:T(8,128)(2,1)} %all-gather.5.cloned.1.call-done), kind=kOutput, calls=%fused_computation.14 | convolution fusion | flops 9663676416 | bytes 22020096 | tf_op jit(solution)/shard_map/dot_general | solution.py:60
  188.1 0.0 copy-start.14
  188.1 0.6 fusion.24
  188.7 0.0 copy-start.9
  188.7 1.1 slice_bitcast_fusion.1
  189.9 0.0 copy-start.7
  189.9 1.2 copy-done.7
  191.1 0.4 fusion.26
  191.6 10.2 %multiply_reduce_fusion = (f32[4,1024]{1,0:T(4,128)S(1)}, f32[4,1024,1536]{2,1,0:T(8,128)}) fusion(bf16[512,4,128]{0,2,1:T(8,128)(2,1)S(1)} %bitcast.104, bf16[1024,4,128]{0,2,1:T(8,128)(2,1)S(1)} %fusion.26, f32[1024,3,4,128]{0,3,2,1:T(8,128)S(1)} %fusion.12, f32[128]{0:T(128)S(1)} %copy-done.9, f32[1024,4]{0,1:T(4,128)S(1)} %add_rsqrt_fusion.1), kind=kOutput, calls=%fused_computation.8 | convolution fusion | flops 1627910144 | bytes 28869120 | tf_op jit(solution)/shard_map/qhd,khd->hqk/dot_general | solution.py:23
  201.8 26.9 %all-gather.9.cloned.1.call-done = bf16[8192,512]{0,1:T(8,128)(2,1)} async-done(((bf16[1024,512]{0,1:T(8,128)(2,1)}), bf16[8192,512]{0,1:T(8,128)(2,1)}) %all-gather.9.cloned.1.call-update) | async-done | bytes 8388624 | tf_op jit(solution)/shard_map/all_gather | solution.py:90
  228.7 52.9 %fusion = (f32[4,1024]{1,0:T(4,128)S(1)}, f32[4,1024,8192]{2,1,0:T(8,128)}) fusion(pred[8192]{0:T(1024)(128)(4,1)S(1)} %fusion.49, bf16[8192,4,128]{0,2,1:T(8,128)(2,1)} %bitcast.98, f32[1024,3,4,128]{0,3,2,1:T(8,128)} %copy-done.1, f32[128]{0:T(128)S(1)} %copy-done.9, f32[1024,4]{0,1:T(4,128)S(1)} %add_rsqrt_fusion.1), kind=kOutput, calls=%fused_computation.2 | convolution fusion | flops 8692166656 | bytes 144744960 | tf_op jit(solution)/shard_map/qhd,khd->hqk/dot_general | solution.py:23
  281.6 41.3 %fusion.1 = f32[4,1024]{1,0:T(4,128)S(1)} fusion(f32[4,1024,8192]{2,1,0:T(8,128)} %get-tuple-element.24, f32[4,1024]{1,0:T(4,128)S(1)} %get-tuple-element.20, pred[8192]{0:T(1024)(128)(4,1)S(1)} %fusion.49), kind=kLoop, calls=%fused_computation.3 | loop fusion | flops 134213632 | bytes 134258688 | tf_op jit(solution)/shard_map/reduce_sum | solution.py:30
  322.9 0.0 all-gather.11.cloned.1.call-done
  322.9 11.9 %copy.51 = bf16[8192,512]{0,1:T(8,128)(2,1)} copy(bf16[8192,512]{1,0:T(8,128)(2,1)} %all-gather.11.cloned.1.call-done) | data formatting | bytes 16777216 | tf_op jit(solution)/shard_map/all_gather | solution.py:93
  334.8 47.0 %fusion.3 = f32[4,1024,128]{1,2,0:T(8,128)} fusion(bf16[8192,4,128]{0,2,1:T(8,128)(2,1)} %bitcast.99, f32[4,1024,8192]{2,1,0:T(8,128)} %get-tuple-element.24, f32[4,1024]{1,0:T(4,128)S(1)} %get-tuple-element.20, pred[8192]{0:T(1024)(128)(4,1)S(1)} %fusion.49), kind=kOutput, calls=%fused_computation.5 | convolution fusion | flops 8724152320 | bytes 144728064 | tf_op jit(solution)/shard_map/hqk,khd->qhd/dot_general | solution.py:31
  381.8 11.6 %fusion.6 = f32[4,1024]{1,0:T(4,128)S(1)} fusion(f32[4,1024,1536]{2,1,0:T(8,128)} %get-tuple-element.22, f32[4,1024]{1,0:T(4,128)S(1)} %get-tuple-element.19), kind=kLoop, calls=%fused_computation.9 | loop fusion | flops 18870272 | bytes 25198592 | tf_op jit(solution)/shard_map/reduce_sum | solution.py:30
  393.4 11.6 %fusion.22 = bf16[1024,4,128]{0,2,1:T(8,128)(2,1)S(1)} fusion(f32[4,1024,128]{1,2,0:T(8,128)} %fusion.3, f32[4,1024,1536]{2,1,0:T(8,128)} %get-tuple-element.22, f32[4,1024]{1,0:T(4,128)S(1)} %get-tuple-element.19, bf16[512,4,128]{0,2,1:T(8,128)(2,1)S(1)} %bitcast.105, bf16[1024,4,128]{0,2,1:T(8,128)(2,1)S(1)} %copy-done.5, ...), kind=kOutput, calls=%fused_computation.31 | convolution fusion | flops 1635254272 | bytes 29949952 | tf_op jit(solution)/shard_map/hqk,khd->qhd/dot_general | solution.py:31
  405.1 5.4 %convolution_convert_fusion = bf16[1024,3072]{1,0:T(8,128)(2,1)} fusion(bf16[1024,512]{0,1:T(8,128)(2,1)S(1)} %bitcast.106, bf16[512,3072]{1,0:T(8,128)(2,1)S(1)} %copy-done), kind=kOutput, calls=%fused_computation.16 | convolution fusion | flops 3224371200 | bytes 10485760 | tf_op jit(solution)/shard_map/dot_general | solution.py:104
  410.5 0.0 reduce-scatter.2.cloned.1.call-update
  410.5 0.6 copy-done.15
  411.1 3.2 slice.30
  414.4 2.7 slice.49
  417.1 3.3 copy.52
  420.4 1.6 mul.164
  421.9 2.9 copy.53
  424.8 2.3 copy.54
  427.1 3.8 multiply_convert_fusion
  430.9 90.6 %reduce-scatter.2.cloned.1.call-done = bf16[256,3072]{1,0:T(8,128)(2,1)} async-done(((bf16[1024,3072]{1,0:T(8,128)(2,1)}), bf16[256,3072]{1,0:T(8,128)(2,1)}) %reduce-scatter.2.cloned.1.call-update) | async-done | bytes 1572880 | tf_op jit(solution)/shard_map/reduce_scatter | solution.py:103
  521.5 3.6 fusion.20
  (36 shorter events, 0.2 us)
Async XLA Ops:
  7.2 397.9 %copy-start = (bf16[512,3072]{1,0:T(8,128)(2,1)S(1)}, bf16[512,3072]{1,0:T(8,128)(2,1)}, u32[]{:S(2)}) copy-start(bf16[512,3072]{1,0:T(8,128)(2,1)} %param.27) | copy-start | bytes 9437188
  7.2 49.0 %all-gather.7.cloned.1.call-start = ((), (), s32[]{:S(2)}) async-start(), calls=%async_computation.2 | async-start | bytes 1179648 | tf_op jit(solution)/shard_map/all_gather | solution.py:80
  14.9 8.7 %copy-start.3 = (bf16[64,3072]{1,0:T(8,128)(2,1)S(1)}, bf16[64,3072]{1,0:T(8,128)(2,1)}, u32[]{:S(2)}) copy-start(bf16[64,3072]{1,0:T(8,128)(2,1)} %param.16) | copy-start | bytes 1179652
  14.9 9.1 %copy-start.11 = (f32[3072]{0:T(1024)S(1)}, f32[3072]{0:T(1024)}, u32[]{:S(2)}) copy-start(f32[3072]{0:T(1024)} %param.21) | copy-start | bytes 36868
  24.0 5.0 copy-start.16
  28.9 5.0 copy-start.12
  28.9 5.0 copy-start.10
  30.0 143.8 %all-gather.5.cloned.1.call-start = ((), (), s32[]{:S(2)}) async-start(), calls=%async_computation.1 | async-start | bytes 7864320 | tf_op jit(solution)/shard_map/all_gather | solution.py:61
  30.0 3.8 copy-start.2
  35.8 192.9 %all-gather.9.cloned.1.call-start = ((), (), s32[]{:S(2)}) async-start(), calls=%async_computation.3 | async-start | bytes 9437184 | tf_op jit(solution)/shard_map/all_gather | solution.py:90
  38.2 284.7 %all-gather.11.cloned.1.call-start = ((), (), s32[]{:S(2)}) async-start(), calls=%async_computation.4 | async-start | bytes 9437184 | tf_op jit(solution)/shard_map/all_gather | solution.py:93
  38.7 482.8 %reduce-scatter.2.cloned.1.call-start = ((), (), s32[]{:S(2)}) async-start(), calls=%async_computation.5 | async-start | bytes 7864320 | tf_op jit(solution)/shard_map/reduce_scatter | solution.py:103
  188.1 3.4 copy-start.1
  188.1 3.0 copy-start.14
  188.7 2.9 copy-start.4
  188.7 2.9 copy-start.9
  189.9 1.2 copy-start.7
  381.8 11.6 %copy-start.5 = (bf16[1024,4,128]{0,2,1:T(8,128)(2,1)S(1)}, bf16[1024,4,128]{0,2,1:T(8,128)(2,1)}, u32[]{:S(2)}) copy-start(bf16[1024,4,128]{0,2,1:T(8,128)(2,1)} %slice_bitcast_fusion.1) | copy-start | bytes 3145732
  381.8 11.7 %copy-start.6 = (bf16[512,1,4,128]{0,3,2,1:T(8,128)(2,1)S(1)}, bf16[512,1,4,128]{0,3,2,1:T(8,128)(2,1)}, u32[]{:S(2)}) copy-start(bf16[512,1,4,128]{0,3,2,1:T(8,128)(2,1)} %copy.62) | copy-start | bytes 1572868
  410.5 0.7 copy-start.15
  414.4 6.0 %copy-start.8 = (f32[1024,4]{0,1:T(4,128)S(1)}, f32[1024,4]{0,1:T(4,128)}, u32[]{:S(2)}) copy-start(f32[1024,4]{0,1:T(4,128)} %copy-done.7) | copy-start | bytes 49156
  427.1 94.4 %copy-start.13 = (f32[3072]{0:T(1024)S(1)}, f32[3072]{0:T(1024)}, u32[]{:S(2)}) copy-start(f32[3072]{0:T(1024)} %param.19) | copy-start | bytes 36868
Sparse Core Ops, SparseCore 0:
  30.1 26.0 all-gather.6
  58.4 115.3 all-gather.4
  176.2 52.4 all-gather.8
  230.4 54.2 all-gather.10
  410.6 110.8 reduce-scatter.1
where the time goes:
time: 533 us; the launch traced here: 532 us
  waiting for transfers between devices  233 us (44%)
  matrix products  146 us (27%)
  local copies, waits for them, and re-layouts  69.7 us (13%)
  other arithmetic  67.7 us (13%)
  between operations  14.1 us (3%)
    all_gather x1, waiting for transfers between devices, per_device(): lax.all_gather(image_mod, 'tensor', axis=0, tiled=True)  111 us
    reduce_scatter x1, waiting for transfers between devices, per_device(): lax.psum_scatter(jnp.dot(attended, out_weight, preferred_element_type=jnp...  90.6 us
    dot_general x2, matrix products, absorb(): jnp.einsum('qhd,khd->hqk', queries, key_rows, preferred_element_type=jnp....  63.1 us
    dot_general x2, matrix products, absorb(): jnp.einsum('hqk,khd->qhd', weights.astype(jnp.bfloat16), value_rows, pref...  58.6 us
    reduce_sum x2, other arithmetic, absorb(): denominator = denominator * rescale + jnp.sum(weights, axis=-1)  52.9 us
    unnamed x40, local copies, waits for them, and re-layouts  31.1 us
    all_gather x1, waiting for transfers between devices, per_device(): lax.all_gather(stale_keys, 'patch', axis=0, tiled=True)  26.9 us
    dot_general x1, matrix products, per_device(): jnp.dot(lax.all_gather(image_mod, 'tensor', axis=0, tiled=True), flat_wei...  14.4 us
  transfers between devices with their start and end apart: 5, of which 4 were waited for; matrix products, arithmetic and copies ran while one was open for 32% of the time, Pallas kernels for 0%

commit v1 on v0

v1 whole, which is shorter than its diff:
```python
from functools import partial

import jax
import jax.numpy as jnp
from jax import lax
from jax.experimental import pallas as pl
from jax.experimental.pallas import tpu as pltpu
from jax.sharding import PartitionSpec as P


def layer_mod(values, shift_vec, scale_vec):
    wide = values.astype(jnp.float32)
    centre = jnp.mean(wide, axis=-1, keepdims=True)
    spread = jnp.mean((wide - centre) * (wide - centre), axis=-1, keepdims=True)
    normed = (wide - centre) * lax.rsqrt(spread + 1e-06)
    return ((1.0 + scale_vec) * normed + shift_vec).astype(jnp.bfloat16)


def rms_gain(values, gain_vec):
    square = jnp.mean(values * values, axis=-1, keepdims=True)
    return values * lax.rsqrt(square + 1e-06) * gain_vec


def attend_body(own_ref, q_ref, fk_ref, fv_ref, tk_ref, tv_ref, sk_ref, sv_ref, o_ref, m_ref, l_ref, acc_ref, *, unit, skip, block, factor):
    rows = q_ref.shape[0]
    m_ref[...] = jnp.full(m_ref.shape, -1e30, jnp.float32)
    l_ref[...] = jnp.zeros(l_ref.shape, jnp.float32)
    acc_ref[...] = jnp.zeros(acc_ref.shape, jnp.float32)

    def absorb(key_rows, value_rows):
        for first in range(0, rows, unit):
            cols = pl.ds(first, unit)
            scores = factor * lax.dot_general(
                key_rows, q_ref[cols, :], (((1,), (1,)), ((), ())), preferred_element_type=jnp.float32
            )
            old_peak = m_ref[:, cols]
            peak = jnp.maximum(old_peak, jnp.max(scores, axis=0, keepdims=True))
            weights = jnp.exp2(scores - peak)
            rescale = jnp.exp2(old_peak - peak)
            m_ref[:, cols] = peak
            l_ref[:, cols] = l_ref[:, cols] * rescale + jnp.sum(weights, axis=0, keepdims=True)
            acc_ref[:, cols] = acc_ref[:, cols] * rescale + lax.dot_general(
                value_rows, weights.astype(jnp.bfloat16), (((0,), (0,)), ((), ())),
                preferred_element_type=jnp.float32,
            )

    def sweep(k_ref, v_ref, jump):
        def step(i, carry):
            start = i * block
            if jump:
                start = start + jnp.where(start >= own_ref[0], skip, 0)
            start = pl.multiple_of(start, block)
            absorb(k_ref[pl.ds(start, block), :], v_ref[pl.ds(start, block), :])
            return carry

        total = k_ref.shape[0] - (skip if jump else 0)
        lax.fori_loop(0, total // block, step, 0)

    sweep(fk_ref, fv_ref, False)
    sweep(tk_ref, tv_ref, False)
    sweep(sk_ref, sv_ref, True)
    o_ref[...] = jnp.transpose(acc_ref[...] / l_ref[...]).astype(jnp.bfloat16)


def attend(own, queries, fk, fv, tk, tv, sk, sv, head_dim):
    rows, feats = queries.shape
    heads = feats // head_dim
    unit = 256 if rows % 256 == 0 else rows
    skip = fk.shape[0]
    block = 512
    for other in (skip, tk.shape[0], sk.shape[0]):
        while other % block:
            block //= 2
    keys = fk.shape[0] + tk.shape[0] + sk.shape[0] - skip
    factor = 1.4426950408889634 / float(head_dim) ** 0.5

    def column(values):
        return pl.BlockSpec((values.shape[0], head_dim), lambda h, own_ref: (0, h))

    def kernel(*refs):
        attend_body(*refs, unit=unit, skip=skip, block=block, factor=factor)

    return pl.pallas_call(
        kernel,
        out_shape=jax.ShapeDtypeStruct((rows, feats), jnp.bfloat16),
        grid_spec=pltpu.PrefetchScalarGridSpec(
            num_scalar_prefetch=1,
            grid=(heads,),
            in_specs=[column(a) for a in (queries, fk, fv, tk, tv, sk, sv)],
            out_specs=column(queries),
            scratch_shapes=[
                pltpu.VMEM((1, rows), jnp.float32),
                pltpu.VMEM((1, rows), jnp.float32),
                pltpu.VMEM((head_dim, rows), jnp.float32),
            ],
        ),
        cost_estimate=pl.CostEstimate(
            flops=4 * rows * keys * feats,
            transcendentals=rows * keys * heads,
            bytes_accessed=4 * (keys + rows) * feats,
        ),
        name="attend",
    )(own, queries, fk, fv, tk, tv, sk, sv)


def per_device(
    tokens, text_tokens, img_shift, img_scale, img_gate, txt_shift, txt_scale, qkv_weight,
    txt_kv_weight, q_gain, k_gain, txt_k_gain, out_weight, stale_keys, stale_values, *, n_patch, n_tensor
):
    width = tokens.shape[1]
    head_dim = q_gain.shape[0]
    feats = qkv_weight.shape[2]
    local_heads = feats // head_dim
    here = lax.axis_index("tensor")
    place = lax.axis_index("patch")
    rows = tokens.shape[0]
    patch_rows = rows * n_tensor
    ahead = [(i, (i + 1) % n_tensor) for i in range(n_tensor)]
    back = [(i, (i - 1) % n_tensor) for i in range(n_tensor)]

    def normed(values, gain_vec):
        split = values.reshape(values.shape[0], local_heads, head_dim)
        return rms_gain(split, gain_vec).astype(jnp.bfloat16).reshape(values.shape)

    key_rows = lax.all_gather(stale_keys, "patch", axis=0, tiled=True)

    image_mods = [layer_mod(tokens, img_shift, img_scale)]
    for _ in range(1, n_tensor):
        image_mods.append(lax.ppermute(image_mods[-1], "tensor", ahead))
    portion = out_weight.shape[0] // n_patch
    moving = lax.dynamic_slice_in_dim(out_weight, place * portion, portion, 0)
    weight_parts = []
    for _ in range(1, n_tensor):
        moving = lax.ppermute(moving, "tensor", back)
        weight_parts.append(moving)

    text_mod = layer_mod(text_tokens, txt_shift, txt_scale)
    text_proj = jnp.dot(
        text_mod, txt_kv_weight.reshape(width, 2 * feats), preferred_element_type=jnp.float32
    )
    text_pairs = jnp.concatenate(
        [normed(text_proj[:, :feats], txt_k_gain), text_proj[:, feats:].astype(jnp.bfloat16)], axis=1
    )
    all_text = lax.all_gather(text_pairs, "patch", axis=0, tiled=True)
    stale_values, all_text = lax.optimization_barrier((stale_values, all_text))
    value_rows = lax.all_gather(stale_values, "patch", axis=0, tiled=True)
    weight_parts, value_rows = lax.optimization_barrier((weight_parts, value_rows))
    weights = [out_weight] + [lax.all_gather(w, "patch", axis=0, tiled=True) for w in weight_parts]

    flat_weight = qkv_weight.reshape(width, 3 * feats)
    queries, fresh_keys, fresh_values = [], [], []
    new_keys = jnp.zeros((patch_rows, feats), jnp.bfloat16)
    new_values = jnp.zeros((patch_rows, feats), jnp.bfloat16)
    for s in range(n_tensor):
        projected = jnp.dot(image_mods[s], flat_weight, preferred_element_type=jnp.float32)
        queries.append(normed(projected[:, :feats], q_gain))
        fresh_keys.append(normed(projected[:, feats : 2 * feats], k_gain))
        fresh_values.append(projected[:, 2 * feats :].astype(jnp.bfloat16))
        at = ((here - s) % n_tensor) * rows
        new_keys = lax.dynamic_update_slice_in_dim(new_keys, fresh_keys[s], at, 0)
        new_values = lax.dynamic_update_slice_in_dim(new_values, fresh_values[s], at, 0)

    own = jnp.reshape(place * patch_rows, (1,)).astype(jnp.int32)
    shared = (new_keys, new_values, all_text[:, :feats], all_text[:, feats:], key_rows, value_rows)
    others = attend(own, jnp.concatenate(queries[1:], axis=0), *shared, head_dim)
    received = []
    for s in range(1, n_tensor):
        to = [(i, (i - s) % n_tensor) for i in range(n_tensor)]
        received.append(lax.ppermute(others[(s - 1) * rows : s * rows], "tensor", to))
    received.insert(0, attend(own, queries[0], *shared, head_dim))
    branch = jnp.zeros((rows, width), jnp.float32)
    for s in range(n_tensor):
        branch = branch + jnp.dot(received[s], weights[s], preferred_element_type=jnp.float32)
    updated = (tokens.astype(jnp.float32) + img_gate * branch).astype(jnp.bfloat16)
    return (updated, new_keys, new_values)


def solution(mesh):
    placed = (
        P(("patch", "tensor"), None),
        P("patch", None),
        P(),
        P(),
        P(),
        P(),
        P(),
        P(None, None, "tensor"),
        P(None, None, "tensor"),
        P(),
        P(),
        P(),
        P("tensor", None),
        P("patch", "tensor"),
        P("patch", "tensor"),
    )
    return jax.shard_map(
        partial(per_device, n_patch=mesh.shape["patch"], n_tensor=mesh.shape["tensor"]),
        mesh=mesh,
        in_specs=placed,
        out_specs=(P(("patch", "tensor"), None), P("patch", "tensor"), P("patch", "tensor")),
        check_vma=False,
    )
```

time: 533 us -> 417 us (0.78)
  Pallas kernels: 0 us -> 130 us
  waiting for transfers between devices: 233 us -> 114 us
  matrix products: 146 us -> 43.5 us
  local copies, waits for them, and re-layouts: 69.7 us -> 48.9 us
  other arithmetic: 67.7 us -> 47.6 us
  starting transfers between devices: 0.38 us -> 15.9 us
    pallas_call x0 -> x2, Pallas kernels: none -> 130 us  [attend(): pl.pallas_call(kernel, out_shape=jax.ShapeDtypeStruct((rows, feats), jnp....]
    all_gather x3 -> x5, waiting for transfers between devices: 138 us -> 19.4 us  [the longest x1 19.3 us: per_device(): value_rows = lax.all_gather(stale_values, 'patch', axis=0, tiled=True)]
    dot_general x7 -> x9, matrix products: 146 us -> 43.5 us  [the longest x4 25.5 us: per_device(): jnp.dot(image_mods[s], flat_weight, preferred_element_type=jnp.float32)]
    reduce_scatter x1 -> x0, waiting for transfers between devices: 90.6 us -> none  [per_device(): lax.psum_scatter(jnp.dot(attended, out_weight, preferred_element_type=jnp...]
    ppermute x0 -> x9, waiting for transfers between devices: none -> 67.6 us  [the longest x3 43.6 us: per_device(): image_mods.append(lax.ppermute(image_mods[-1], 'tensor', ahead))]
    reduce_sum x2 -> x0, other arithmetic: 52.9 us -> none  [absorb(): denominator = denominator * rescale + jnp.sum(weights, axis=-1)]
    all_gather x1, waiting for transfers between devices: 4.44 us -> 26.2 us  [per_device(): all_text = lax.all_gather(text_pairs, 'patch', axis=0, tiled=True)]
    mul x0 -> x9, local copies, waits for them, and re-layouts: none -> 17.2 us  [rms_gain(): square = jnp.mean(values * values, axis=-1, keepdims=True)]
  transfers between devices with their start and end apart: 5 -> 15, of which waited for: 4 -> 8; matrix products, arithmetic and copies ran while one was open for 32% -> 28% of each run, Pallas kernels for 0% -> 31%
where the time goes in v1:
time: 417 us; the launch traced here: 415 us
  Pallas kernels  130 us (31%)
  waiting for transfers between devices  114 us (27%)
  local copies, waits for them, and re-layouts  48.9 us (12%)
  other arithmetic  47.6 us (11%)
  matrix products  43.5 us (10%)
  starting transfers between devices  15.9 us (4%)
  between operations  14.6 us (4%)
    pallas_call x2, Pallas kernels, attend(): pl.pallas_call(kernel, out_shape=jax.ShapeDtypeStruct((rows, feats), jnp....  130 us
    ppermute x3, waiting for transfers between devices, per_device(): image_mods.append(lax.ppermute(image_mods[-1], 'tensor', ahead))  43.6 us
    all_gather x1, waiting for transfers between devices, per_device(): all_text = lax.all_gather(text_pairs, 'patch', axis=0, tiled=True)  26.2 us
    dot_general x4, matrix products, per_device(): jnp.dot(image_mods[s], flat_weight, preferred_element_type=jnp.float32)  25.5 us
    ppermute x3, waiting for transfers between devices, per_device(): moving = lax.ppermute(moving, 'tensor', back)  24 us
    unnamed x38, local copies, waits for them, and re-layouts  21.3 us
    all_gather x1, waiting for transfers between devices, per_device(): value_rows = lax.all_gather(stale_values, 'patch', axis=0, tiled=True)  19.3 us
    mul x9, local copies, waits for them, and re-layouts, rms_gain(): square = jnp.mean(values * values, axis=-1, keepdims=True)  17.2 us
  transfers between devices with their start and end apart: 15, of which 8 were waited for; matrix products, arithmetic and copies ran while one was open for 28% of the time, Pallas kernels for 31%

profile of v1, /device:TPU:0, one launch (start us, length us, event | category | flops | bytes accessed | tf_op | source)
XLA Modules:
  0.0 414.8 jit_solution(8175786956440883042)
XLA Ops:
  7.2 1.3 convert_reduce_fusion.1
  8.5 1.3 fusion.11
  9.9 4.9 %copy.53 = bf16[384,8,2,512]{3,1,2,0:T(8,128)(2,1)S(1)} copy(bf16[384,8,2,512]{3,2,1,0:T(2,128)(2,1)} %bitcast.103) | data formatting | bytes 12582912
  14.8 1.3 fusion.31
  20.0 1.5 pad_maximum_fusion.1
  21.6 26.2 %all-gather.7.cloned.1.call-done = bf16[512,1024]{1,0:T(8,128)(2,1)} async-done(((bf16[64,1024]{1,0:T(8,128)(2,1)}), bf16[512,1024]{1,0:T(8,128)(2,1)}) %all-gather.7.cloned.1.call-update) | async-done | bytes 1048592 | tf_op jit(solution)/shard_map/all_gather | solution.py:144
  48.7 3.4 collective-permute-start.3
  52.1 8.8 %collective-permute-done.3 = bf16[64,3072]{1,0:T(8,128)(2,1)} collective-permute-done((bf16[64,3072]{1,0:T(8,128)(2,1)S(1)}, bf16[64,3072]{1,0:T(8,128)(2,1)}, u32[]{:S(2)}, u32[]{:S(2)}) %collective-permute-start.3) | collective-permute-done | bytes 393248 | tf_op jit(solution)/shard_map/ppermute | solution.py:134
  60.8 4.4 %collective-permute-start.4 = (bf16[64,3072]{1,0:T(8,128)(2,1)}, bf16[64,3072]{1,0:T(8,128)(2,1)S(1)}, u32[]{:S(2)}, u32[]{:S(2)}) collective-permute-start(bf16[64,3072]{1,0:T(8,128)(2,1)} %collective-permute-done.3), channel_id=1, source_target_pairs={{0,3},{1,0},{2,1},{3,2},{4,7},{5,4},{6,5},{7,6},{8,11},{9,8},{10,9... | collective-permute-start | bytes 1179656 | tf_op jit(solution)/shard_map/ppermute | solution.py:134
  65.2 8.2 %collective-permute-done.4 = bf16[64,3072]{1,0:T(8,128)(2,1)S(1)} collective-permute-done((bf16[64,3072]{1,0:T(8,128)(2,1)}, bf16[64,3072]{1,0:T(8,128)(2,1)S(1)}, u32[]{:S(2)}, u32[]{:S(2)}) %collective-permute-start.4) | collective-permute-done | bytes 393248 | tf_op jit(solution)/shard_map/ppermute | solution.py:134
  73.4 4.2 %collective-permute-start.5 = (bf16[64,3072]{1,0:T(8,128)(2,1)S(1)}, bf16[64,3072]{1,0:T(8,128)(2,1)}, u32[]{:S(2)}, u32[]{:S(2)}) collective-permute-start(bf16[64,3072]{1,0:T(8,128)(2,1)S(1)} %collective-permute-done.4), channel_id=1, source_target_pairs={{0,3},{1,0},{2,1},{3,2},{4,7},{5,4},{6,5},{7,6},{8,11},{9,8},{10,9... | collective-permute-start | bytes 1179656 | tf_op jit(solution)/shard_map/ppermute | solution.py:134
  77.6 7.1 %collective-permute-done.5 = bf16[64,3072]{1,0:T(8,128)(2,1)} collective-permute-done((bf16[64,3072]{1,0:T(8,128)(2,1)S(1)}, bf16[64,3072]{1,0:T(8,128)(2,1)}, u32[]{:S(2)}, u32[]{:S(2)}) %collective-permute-start.5) | collective-permute-done | bytes 393248 | tf_op jit(solution)/shard_map/ppermute | solution.py:134
  84.7 19.3 %all-gather.11.cloned.1.call-done.refs_7_ = bf16[8192,512]{1,0:T(8,128)(2,1)} async-done(((bf16[1024,512]{1,0:T(8,128)(2,1)}), bf16[8192,512]{1,0:T(8,128)(2,1)}) %all-gather.11.cloned.1.call-update) | async-done | bytes 8388624 | tf_op jit(solution)/shard_map/all_gather | solution.py:146
  104.1 1.8 convert_reduce_fusion
  105.9 2.0 fusion.5
  107.9 1.9 fusion.8
  109.9 1.5 collective-permute-start
  111.3 12.9 %copy.29 = bf16[3072,3,512]{0,2,1:T(8,128)(2,1)} copy(bf16[3072,3,512]{2,0,1:T(8,128)(2,1)} %param.22) | data formatting | bytes 18874368 | tf_op args[7]
  124.3 8.0 %fusion.49 = f32[256,1536]{1,0:T(8,128)} fusion(bf16[256,3072]{1,0:T(8,128)(2,1)} %fusion.8, bf16[3072,1536]{0,1:T(8,128)(2,1)} %bitcast.99), kind=kOutput, calls=%fused_computation.99 | convolution fusion | flops 2415919104 | bytes 12582912 | tf_op jit(solution)/shard_map/dot_general | solution.py:155
  132.2 1.9 slice_multiply_fusion.7
  134.1 2.2 mul.306
  136.3 1.4 reduce_sum.119
  137.9 1.0 broadcast.194.clone
  138.9 1.8 fusion.37
  140.7 7.8 %collective-permute-done = bf16[256,3072]{1,0:T(8,128)(2,1)} collective-permute-done((bf16[256,3072]{1,0:T(8,128)(2,1)}, bf16[256,3072]{1,0:T(8,128)(2,1)}, u32[]{:S(2)}, u32[]{:S(2)}) %collective-permute-start) | collective-permute-done | bytes 1572896 | tf_op jit(solution)/shard_map/ppermute | solution.py:129
  148.5 5.7 %fusion.50 = f32[256,1536]{1,0:T(8,128)S(1)} fusion(bf16[256,3072]{1,0:T(8,128)(2,1)} %collective-permute-done, bf16[3072,1536]{0,1:T(8,128)(2,1)} %bitcast.100), kind=kOutput, calls=%fused_computation.100 | convolution fusion | flops 2415919104 | bytes 12582912 | tf_op jit(solution)/shard_map/dot_general | solution.py:155
  154.3 1.1 copy-done.5
  156.2 2.0 mul.361
  158.3 1.4 reduce_sum.127
  160.6 2.8 slice_multiply_fusion.5
  163.4 2.0 mul.315
  165.4 1.4 reduce_sum.120
  166.8 2.0 mul.325
  168.8 2.1 reduce_sum.121
  170.9 1.1 add_rsqrt_fusion.5
  172.3 1.0 broadcast.194.clone.1
  173.4 1.8 fusion.41
  177.6 20.1 %collective-permute-done.1 = bf16[256,3072]{1,0:T(8,128)(2,1)} collective-permute-done((bf16[256,3072]{1,0:T(8,128)(2,1)}, bf16[256,3072]{1,0:T(8,128)(2,1)}, u32[]{:S(2)}, u32[]{:S(2)}) %collective-permute-start.1) | collective-permute-done | bytes 1572896 | tf_op jit(solution)/shard_map/ppermute | solution.py:129
  197.7 5.7 %fusion.51 = f32[256,1536]{1,0:T(8,128)S(1)} fusion(bf16[256,3072]{1,0:T(8,128)(2,1)} %collective-permute-done.1, bf16[3072,1536]{0,1:T(8,128)(2,1)} %bitcast.101), kind=kOutput, calls=%fused_computation.101 | convolution fusion | flops 2415919104 | bytes 12582912 | tf_op jit(solution)/shard_map/dot_general | solution.py:155
  203.4 1.1 copy-done.4
  205.4 2.0 mul.367
  207.5 1.4 reduce_sum.128
  209.2 2.3 slice_multiply_fusion.4
  211.5 2.0 mul.332
  213.5 2.0 reduce_sum.122
  216.9 2.1 fusion.39
  219.0 15.6 %collective-permute-done.2 = bf16[256,3072]{1,0:T(8,128)(2,1)} collective-permute-done((bf16[256,3072]{1,0:T(8,128)(2,1)}, bf16[256,3072]{1,0:T(8,128)(2,1)}, u32[]{:S(2)}, u32[]{:S(2)}) %collective-permute-start.2) | collective-permute-done | bytes 1572896 | tf_op jit(solution)/shard_map/ppermute | solution.py:129
  234.6 6.1 %fusion.52 = f32[256,1536]{1,0:T(8,128)S(1)} fusion(bf16[256,3072]{1,0:T(8,128)(2,1)} %collective-permute-done.2, bf16[3072,1536]{0,1:T(8,128)(2,1)} %bitcast.102), kind=kOutput, calls=%fused_computation.102 | convolution fusion | flops 2415919104 | bytes 12582912 | tf_op jit(solution)/shard_map/dot_general | solution.py:155
  240.7 1.1 copy-done.3
  242.7 2.0 mul.373
  244.7 1.4 reduce_sum.129
  246.5 2.3 slice_multiply_fusion.3
  248.8 2.0 mul.339
  250.8 1.4 reduce_sum.123
  252.2 2.0 pad_maximum_fusion.refs_1_
  254.6 2.2 fusion.40
  256.7 91.8 %attend.3 = bf16[768,512]{1,0:T(8,128)(2,1)} custom-call(s32[1]{0:T(128)} %bitcast.refs_0_, bf16[768,512]{1,0:T(8,128)(2,1)} %pad_maximum_fusion.refs_1_, bf16[1024,512]{1,0:T(8,128)(2,1)} %get-tuple-element.18.refs_2_, bf16[1024,512]{1,0:T(8,128)(2,1)} %get-tuple-element.17.refs_3_, bf16[512,512]{1,0:T(8,128)(2,1)} %get-tuple-element.30.refs_4_, ...), custom_call_target="tpu_custom_call" | custom-call | flops 13690208256 | bytes 19398656 | tf_op jit(solution)/shard_map/attend/pallas_call | solution.py:83
  348.5 2.0 fusion.48
  350.5 2.0 collective-permute-start.8
  352.5 38.6 %attend.2 = bf16[256,512]{1,0:T(8,128)(2,1)} custom-call(s32[1]{0:T(128)} %bitcast.refs_0_, bf16[256,512]{1,0:T(8,128)(2,1)} %get-tuple-element.35.refs_1_, bf16[1024,512]{1,0:T(8,128)(2,1)} %get-tuple-element.18.refs_2_, bf16[1024,512]{1,0:T(8,128)(2,1)} %get-tuple-element.17.refs_3_, bf16[512,512]{1,0:T(8,128)(2,1)} %get-tuple-element.30.refs_4_, ...), custom_call_target="tpu_custom_call" | custom-call | flops 4563402752 | bytes 18350080 | tf_op jit(solution)/shard_map/attend/pallas_call | solution.py:83
  391.2 3.0 fusion.53
  394.2 2.7 convolution_add_fusion.1
  396.9 4.6 %fusion.54 = f32[256,3072]{1,0:T(8,128)} fusion(bf16[256,512]{1,0:T(8,128)(2,1)} %collective-permute-done.8, bf16[512,3072]{1,0:T(8,128)(2,1)} %all-gather.17.cloned.1.call-done), kind=kOutput, calls=%fused_computation.104 | convolution fusion | flops 805306368 | bytes 6553600 | tf_op jit(solution)/shard_map/dot_general | solution.py:173
  401.5 6.5 %fusion.2 = bf16[256,3072]{1,0:T(8,128)(2,1)} fusion(f32[256,3072]{1,0:T(8,128)} %fusion.54, f32[256,3072]{1,0:T(8,128)} %convolution_add_fusion.1, bf16[256,512]{1,0:T(8,128)(2,1)} %collective-permute-done.7, bf16[512,3072]{1,0:T(8,128)(2,1)} %all-gather.15.cloned.1.call-done, bf16[256,3072]{1,0:T(8,128)(2,1)} %param.15, f32[3072]{0:T(1024)S(1)} %copy-done.11), kind=kOutput, calls=%fused_computation.7 | convolution fusion | flops 810024960 | bytes 12857344 | tf_op jit(solution)/shard_map/dot_general | solution.py:173
  (93 shorter events, 13.7 us)
Async XLA Ops:
  7.2 41.5 %copy-start = (bf16[512,3072]{1,0:T(8,128)(2,1)S(1)}, bf16[512,3072]{1,0:T(8,128)(2,1)}, u32[]{:S(2)}) copy-start(bf16[512,3072]{1,0:T(8,128)(2,1)} %param.27) | copy-start | bytes 9437188
  7.2 40.6 %all-gather.7.cloned.1.call-start = ((), (), s32[]{:S(2)}) async-start(), calls=%async_computation | async-start | bytes 1179648 | tf_op jit(solution)/shard_map/all_gather | solution.py:144
  9.8 4.9 %copy-start.12 = (f32[3072]{0:T(1024)S(1)}, f32[3072]{0:T(1024)}, u32[]{:S(2)}) copy-start(f32[3072]{0:T(1024)} %param.21) | copy-start | bytes 36868
  9.8 4.9 %copy-start.2 = (bf16[64,3072]{1,0:T(8,128)(2,1)S(1)}, bf16[64,3072]{1,0:T(8,128)(2,1)}, u32[]{:S(2)}) copy-start(bf16[64,3072]{1,0:T(8,128)(2,1)} %param.16) | copy-start | bytes 1179652
  9.8 4.9 %copy-start.14 = (f32[3072]{0:T(1024)S(1)}, f32[3072]{0:T(1024)}, u32[]{:S(2)}) copy-start(f32[3072]{0:T(1024)} %param.20) | copy-start | bytes 36868
  14.8 5.1 %copy-start.15 = (f32[128]{0:T(128)S(1)}, f32[128]{0:T(128)}, u32[]{:S(2)}) copy-start(f32[128]{0:T(128)} %param.26) | copy-start | bytes 1540
  21.6 86.3 %copy-start.10 = (f32[3072]{0:T(1024)S(1)}, f32[3072]{0:T(1024)}, u32[]{:S(2)}) copy-start(f32[3072]{0:T(1024)} %param.17) | copy-start | bytes 36868
  21.6 82.4 %all-gather.11.cloned.1.call-start = ((), (), s32[]{:S(2)}) async-start(), calls=%async_computation.2 | async-start | bytes 9437184 | tf_op jit(solution)/shard_map/all_gather | solution.py:146
  47.8 208.9 %all-gather.9.cloned.1.call-start = ((), (), s32[]{:S(2)}) async-start(), calls=%async_computation.1 | async-start | bytes 9437184 | tf_op jit(solution)/shard_map/all_gather | solution.py:125
  48.6 342.6 %all-gather.13.cloned.1.call-start = ((), (), s32[]{:S(2)}) async-start(), calls=%async_computation.3 | async-start | bytes 3538944 | tf_op jit(solution)/shard_map/all_gather | solution.py:148
  48.7 12.1 %collective-permute-start.3 = (bf16[64,3072]{1,0:T(8,128)(2,1)S(1)}, bf16[64,3072]{1,0:T(8,128)(2,1)}, u32[]{:S(2)}, u32[]{:S(2)}) collective-permute-start(bf16[64,3072]{1,0:T(8,128)(2,1)S(1)} %constant_dynamic-slice_fusion), channel_id=1, source_target_pairs={{0,3},{1,0},{2,1},{3,2},{4,7},{5,4},{6,5},{7,6},{8,11},{9,8},{10,9... | collective-permute-start | bytes 1179656 | tf_op jit(solution)/shard_map/ppermute | solution.py:134
  60.8 12.6 %collective-permute-start.4 = (bf16[64,3072]{1,0:T(8,128)(2,1)}, bf16[64,3072]{1,0:T(8,128)(2,1)S(1)}, u32[]{:S(2)}, u32[]{:S(2)}) collective-permute-start(bf16[64,3072]{1,0:T(8,128)(2,1)} %collective-permute-done.3), channel_id=1, source_target_pairs={{0,3},{1,0},{2,1},{3,2},{4,7},{5,4},{6,5},{7,6},{8,11},{9,8},{10,9... | collective-permute-start | bytes 1179656 | tf_op jit(solution)/shard_map/ppermute | solution.py:134
  73.4 36.4 %copy-start.9 = (bf16[64,3072]{1,0:T(8,128)(2,1)}, bf16[64,3072]{1,0:T(8,128)(2,1)S(1)}, u32[]{:S(2)}) copy-start(bf16[64,3072]{1,0:T(8,128)(2,1)S(1)} %collective-permute-done.4) | copy-start | bytes 1179652
  73.4 11.2 %collective-permute-start.5 = (bf16[64,3072]{1,0:T(8,128)(2,1)S(1)}, bf16[64,3072]{1,0:T(8,128)(2,1)}, u32[]{:S(2)}, u32[]{:S(2)}) collective-permute-start(bf16[64,3072]{1,0:T(8,128)(2,1)S(1)} %collective-permute-done.4), channel_id=1, source_target_pairs={{0,3},{1,0},{2,1},{3,2},{4,7},{5,4},{6,5},{7,6},{8,11},{9,8},{10,9... | collective-permute-start | bytes 1179656 | tf_op jit(solution)/shard_map/ppermute | solution.py:134
  104.0 292.9 %all-gather.17.cloned.1.call-start = ((), (), s32[]{:S(2)}) async-start(), calls=%async_computation.5 | async-start | bytes 3538944 | tf_op jit(solution)/shard_map/all_gather | solution.py:148
  104.1 3.8 copy-start.13
  104.1 3.8 copy-start.1
  109.9 38.7 %collective-permute-start = (bf16[256,3072]{1,0:T(8,128)(2,1)}, bf16[256,3072]{1,0:T(8,128)(2,1)}, u32[]{:S(2)}, u32[]{:S(2)}) collective-permute-start(bf16[256,3072]{1,0:T(8,128)(2,1)} %fusion.8), channel_id=1, source_target_pairs={{0,1},{1,2},{2,3},{3,0},{4,5},{5,6},{6,7},{7,4},{8,9},{9,10},{10,1... | collective-permute-start | bytes 4718600 | tf_op jit(solution)/shard_map/ppermute | solution.py:129
  132.2 5.6 %copy-start.16 = (f32[128]{0:T(128)S(1)}, f32[128]{0:T(128)}, u32[]{:S(2)}) copy-start(f32[128]{0:T(128)} %param.24) | copy-start | bytes 1540
  132.2 5.6 %copy-start.17 = (f32[128]{0:T(128)S(1)}, f32[128]{0:T(128)}, u32[]{:S(2)}) copy-start(f32[128]{0:T(128)} %param.25) | copy-start | bytes 1540
  137.7 263.8 %all-gather.15.cloned.1.call-start = ((), (), s32[]{:S(2)}) async-start(), calls=%async_computation.4 | async-start | bytes 3538944 | tf_op jit(solution)/shard_map/all_gather | solution.py:148
  154.2 1.1 copy-start.5
  159.7 38.0 %collective-permute-start.1 = (bf16[256,3072]{1,0:T(8,128)(2,1)}, bf16[256,3072]{1,0:T(8,128)(2,1)}, u32[]{:S(2)}, u32[]{:S(2)}) collective-permute-start(bf16[256,3072]{1,0:T(8,128)(2,1)} %collective-permute-done), channel_id=1, source_target_pairs={{0,1},{1,2},{2,3},{3,0},{4,5},{5,6},{6,7},{7,4},{8,9},{9,10},{10,1... | collective-permute-start | bytes 4718600 | tf_op jit(solution)/shard_map/ppermute | solution.py:129
  170.9 4.7 %copy-start.6 = (f32[256,1536]{1,0:T(8,128)S(1)}, f32[256,1536]{1,0:T(8,128)}, u32[]{:S(2)}) copy-start(f32[256,1536]{1,0:T(8,128)} %copy-done.5) | copy-start | bytes 4718596
  170.9 5.6 %copy-start.8 = (bf16[512,1024]{1,0:T(8,128)(2,1)S(1)}, bf16[512,1024]{1,0:T(8,128)(2,1)}, u32[]{:S(2)}) copy-start(bf16[512,1024]{1,0:T(8,128)(2,1)} %all-gather.7.cloned.1.call-done) | copy-start | bytes 3145732
  197.7 36.9 %collective-permute-start.2 = (bf16[256,3072]{1,0:T(8,128)(2,1)}, bf16[256,3072]{1,0:T(8,128)(2,1)}, u32[]{:S(2)}, u32[]{:S(2)}) collective-permute-start(bf16[256,3072]{1,0:T(8,128)(2,1)} %collective-permute-done.1), channel_id=1, source_target_pairs={{0,1},{1,2},{2,3},{3,0},{4,5},{5,6},{6,7},{7,4},{8,9},{9,10},{10,1... | collective-permute-start | bytes 4718600 | tf_op jit(solution)/shard_map/ppermute | solution.py:129
  203.4 1.1 copy-start.4
  240.7 1.1 copy-start.3
  350.5 40.6 %collective-permute-start.6 = (bf16[256,512]{1,0:T(8,128)(2,1)}, bf16[256,512]{1,0:T(8,128)(2,1)}, u32[]{:S(2)}, u32[]{:S(2)}) collective-permute-start(bf16[256,512]{1,0:T(8,128)(2,1)} %get-tuple-element.33), channel_id=1, source_target_pairs={{0,3},{1,0},{2,1},{3,2},{4,7},{5,4},{6,5},{7,6},{8,11},{9,8},{10,9... | collective-permute-start | bytes 786440 | tf_op jit(solution)/shard_map/ppermute | solution.py:169
  350.5 46.4 %collective-permute-start.8 = (bf16[256,512]{1,0:T(8,128)(2,1)}, bf16[256,512]{1,0:T(8,128)(2,1)}, u32[]{:S(2)}, u32[]{:S(2)}) collective-permute-start(bf16[256,512]{1,0:T(8,128)(2,1)} %get-tuple-element.32), channel_id=1, source_target_pairs={{0,1},{1,2},{2,3},{3,0},{4,5},{5,6},{6,7},{7,4},{8,9},{9,10},{10,1... | collective-permute-start | bytes 786440 | tf_op jit(solution)/shard_map/ppermute | solution.py:169
  352.5 49.0 %collective-permute-start.7 = (bf16[256,512]{1,0:T(8,128)(2,1)}, bf16[256,512]{1,0:T(8,128)(2,1)}, u32[]{:S(2)}, u32[]{:S(2)}) collective-permute-start(bf16[256,512]{1,0:T(8,128)(2,1)} %get-tuple-element.31), channel_id=1, source_target_pairs={{0,2},{1,3},{2,0},{3,1},{4,6},{5,7},{6,4},{7,5},{8,10},{9,11},{10,... | collective-permute-start | bytes 786440 | tf_op jit(solution)/shard_map/ppermute | solution.py:169
  391.1 3.0 copy-start.7
  396.9 4.6 %copy-start.11 = (f32[3072]{0:T(1024)S(1)}, f32[3072]{0:T(1024)}, u32[]{:S(2)}) copy-start(f32[3072]{0:T(1024)} %param.19) | copy-start | bytes 36868
Sparse Core Ops, SparseCore 0:
  21.7 26.0 all-gather.6
  49.7 54.2 all-gather.10
  105.9 54.2 all-gather.8
  161.9 32.1 all-gather.12
  195.8 32.1 all-gather.16
  229.8 32.1 all-gather.14

commit v2 on v1

--- a/solution.py
+++ b/solution.py
@@ -27,34 +27,45 @@
     l_ref[...] = jnp.zeros(l_ref.shape, jnp.float32)
     acc_ref[...] = jnp.zeros(acc_ref.shape, jnp.float32)
 
-    def absorb(key_rows, value_rows):
-        for first in range(0, rows, unit):
-            cols = pl.ds(first, unit)
-            scores = factor * lax.dot_general(
-                key_rows, q_ref[cols, :], (((1,), (1,)), ((), ())), preferred_element_type=jnp.float32
-            )
-            old_peak = m_ref[:, cols]
-            peak = jnp.maximum(old_peak, jnp.max(scores, axis=0, keepdims=True))
-            weights = jnp.exp2(scores - peak)
-            rescale = jnp.exp2(old_peak - peak)
-            m_ref[:, cols] = peak
-            l_ref[:, cols] = l_ref[:, cols] * rescale + jnp.sum(weights, axis=0, keepdims=True)
-            acc_ref[:, cols] = acc_ref[:, cols] * rescale + lax.dot_general(
-                value_rows, weights.astype(jnp.bfloat16), (((0,), (0,)), ((), ())),
-                preferred_element_type=jnp.float32,
-            )
+    def score(k_ref, at, first):
+        return factor * lax.dot_general(
+            k_ref[pl.ds(at, block), :], q_ref[pl.ds(first, unit), :],
+            (((1,), (1,)), ((), ())), preferred_element_type=jnp.float32,
+        )
+
+    def absorb(scores, v_ref, at, first):
+        cols = pl.ds(first, unit)
+        old_peak = m_ref[:, cols]
+        peak = jnp.maximum(old_peak, jnp.max(scores, axis=0, keepdims=True))
+        weights = jnp.exp2(scores - peak)
+        rescale = jnp.exp2(old_peak - peak)
+        m_ref[:, cols] = peak
+        l_ref[:, cols] = l_ref[:, cols] * rescale + jnp.sum(weights, axis=0, keepdims=True)
+        acc_ref[:, cols] = acc_ref[:, cols] * rescale + lax.dot_general(
+            v_ref[pl.ds(at, block), :], weights.astype(jnp.bfloat16),
+            (((0,), (0,)), ((), ())), preferred_element_type=jnp.float32,
+        )
 
     def sweep(k_ref, v_ref, jump):
+        total = k_ref.shape[0] - (skip if jump else 0)
+        pieces = 2 if total % (2 * block) == 0 and skip % (2 * block) == 0 else 1
+        stride = pieces * block
+
         def step(i, carry):
-            start = i * block
+            start = i * stride
             if jump:
                 start = start + jnp.where(start >= own_ref[0], skip, 0)
-            start = pl.multiple_of(start, block)
-            absorb(k_ref[pl.ds(start, block), :], v_ref[pl.ds(start, block), :])
+            start = pl.multiple_of(start, stride)
+            items = [(start + p * block, f) for p in range(pieces) for f in range(0, rows, unit)]
+            ready = score(k_ref, *items[0])
+            for n, item in enumerate(items):
+                scores = ready
+                if n + 1 < len(items):
+                    ready = score(k_ref, *items[n + 1])
+                absorb(scores, v_ref, *item)
             return carry
 
-        total = k_ref.shape[0] - (skip if jump else 0)
-        lax.fori_loop(0, total // block, step, 0)
+        lax.fori_loop(0, total // stride, step, 0)
 
     sweep(fk_ref, fv_ref, False)
     sweep(tk_ref, tv_ref, False)
@@ -125,10 +136,24 @@
     key_rows = lax.all_gather(stale_keys, "patch", axis=0, tiled=True)
 
     image_mods = [layer_mod(tokens, img_shift, img_scale)]
-    for _ in range(1, n_tensor):
-        image_mods.append(lax.ppermute(image_mods[-1], "tensor", ahead))
+    text_tokens, image_mods[0] = lax.optimization_barrier((text_tokens, image_mods[0]))
+    flat_weight = qkv_weight.reshape(width, 3 * feats)
+    queries, fresh_keys, fresh_values = [], [], []
+    for s in range(n_tensor):
+        if s + 1 < n_tensor:
+            sent = image_mods[s]
+            if s:
+                sent, queries[-1], fresh_keys[-1] = lax.optimization_barrier(
+                    (sent, queries[-1], fresh_keys[-1])
+                )
+            image_mods.append(lax.ppermute(sent, "tensor", ahead))
+        projected = jnp.dot(image_mods[s], flat_weight, preferred_element_type=jnp.float32)
+        queries.append(normed(projected[:, :feats], q_gain))
+        fresh_keys.append(normed(projected[:, feats : 2 * feats], k_gain))
+        fresh_values.append(projected[:, 2 * feats :].astype(jnp.bfloat16))
     portion = out_weight.shape[0] // n_patch
     moving = lax.dynamic_slice_in_dim(out_weight, place * portion, portion, 0)
+    moving, image_mods[-1] = lax.optimization_barrier((moving, image_mods[-1]))
     weight_parts = []
     for _ in range(1, n_tensor):
         moving = lax.ppermute(moving, "tensor", back)
@@ -144,18 +169,11 @@
     all_text = lax.all_gather(text_pairs, "patch", axis=0, tiled=True)
     stale_values, all_text = lax.optimization_barrier((stale_values, all_text))
     value_rows = lax.all_gather(stale_values, "patch", axis=0, tiled=True)
-    weight_parts, value_rows = lax.optimization_barrier((weight_parts, value_rows))
     weights = [out_weight] + [lax.all_gather(w, "patch", axis=0, tiled=True) for w in weight_parts]
 
-    flat_weight = qkv_weight.reshape(width, 3 * feats)
-    queries, fresh_keys, fresh_values = [], [], []
     new_keys = jnp.zeros((patch_rows, feats), jnp.bfloat16)
     new_values = jnp.zeros((patch_rows, feats), jnp.bfloat16)
     for s in range(n_tensor):
-        projected = jnp.dot(image_mods[s], flat_weight, preferred_element_type=jnp.float32)
-        queries.append(normed(projected[:, :feats], q_gain))
-        fresh_keys.append(normed(projected[:, feats : 2 * feats], k_gain))
-        fresh_values.append(projected[:, 2 * feats :].astype(jnp.bfloat16))
         at = ((here - s) % n_tensor) * rows
         new_keys = lax.dynamic_update_slice_in_dim(new_keys, fresh_keys[s], at, 0)
         new_values = lax.dynamic_update_slice_in_dim(new_values, fresh_values[s], at, 0)

time: 417 us -> 378 us (0.906)
  Pallas kernels: 130 us -> 83.4 us
  waiting for transfers between devices: 114 us -> 134 us
  other arithmetic: 47.6 us -> 37.1 us
  local copies, waits for them, and re-layouts: 48.9 us -> 53.2 us
    pallas_call x2, Pallas kernels: 130 us -> 83.4 us  [attend(): pl.pallas_call(kernel, out_shape=jax.ShapeDtypeStruct((rows, feats), jnp....]
    ppermute x3, waiting for transfers between devices: 43.6 us -> 85.9 us  [per_device(): image_mods.append(lax.ppermute(sent, 'tensor', ahead))]
    all_gather x1, waiting for transfers between devices: 19.3 us -> 0.01 us  [per_device(): value_rows = lax.all_gather(stale_values, 'patch', axis=0, tiled=True)]
    ppermute x3, starting transfers between devices: 11.9 us -> 5.03 us  [per_device(): moving = lax.ppermute(moving, 'tensor', back)]
    mul x8 -> x7, other arithmetic: 12.5 us -> 8.46 us  [rms_gain(): square = jnp.mean(values * values, axis=-1, keepdims=True)]
    unnamed x38 -> x44, local copies, waits for them, and re-layouts: 21.3 us -> 23 us
  transfers between devices with their start and end apart: 15 -> 15, of which waited for: 8 -> 7; matrix products, arithmetic and copies ran while one was open for 28% -> 28% of each run, Pallas kernels for 31% -> 22%
where the time goes in v2:
time: 378 us; the launch traced here: 376 us
  waiting for transfers between devices  134 us (35%)
  Pallas kernels  83.4 us (22%)
  local copies, waits for them, and re-layouts  53.2 us (14%)
  matrix products  41 us (11%)
  other arithmetic  37.1 us (10%)
  between operations  14.7 us (4%)
  starting transfers between devices  12.2 us (3%)
    ppermute x3, waiting for transfers between devices, per_device(): image_mods.append(lax.ppermute(sent, 'tensor', ahead))  85.9 us
    pallas_call x2, Pallas kernels, attend(): pl.pallas_call(kernel, out_shape=jax.ShapeDtypeStruct((rows, feats), jnp....  83.4 us
    all_gather x1, waiting for transfers between devices, per_device(): all_text = lax.all_gather(text_pairs, 'patch', axis=0, tiled=True)  25.4 us
    unnamed x44, local copies, waits for them, and re-layouts  23 us
    dot_general x4, matrix products, per_device(): jnp.dot(image_mods[s], flat_weight, preferred_element_type=jnp.float32)  23 us
    ppermute x3, waiting for transfers between devices, per_device(): moving = lax.ppermute(moving, 'tensor', back)  22 us
    dot_general x4, matrix products, per_device(): jnp.dot(received[s], weights[s], preferred_element_type=jnp.float32)  16.8 us
    mul x9, local copies, waits for them, and re-layouts, rms_gain(): square = jnp.mean(values * values, axis=-1, keepdims=True)  16.2 us
  transfers between devices with their start and end apart: 15, of which 7 were waited for; matrix products, arithmetic and copies ran while one was open for 28% of the time, Pallas kernels for 22%

profile of v2, /device:TPU:0, one launch (start us, length us, event | category | flops | bytes accessed | tf_op | source)
XLA Modules:
  0.0 375.8 jit_solution(6491734781755127949)
XLA Ops:
  7.3 1.8 convert_reduce_fusion
  9.1 2.0 fusion.5
  11.2 1.9 fusion.8
  13.6 4.8 %copy.54 = bf16[384,8,2,512]{3,1,2,0:T(8,128)(2,1)S(1)} copy(bf16[384,8,2,512]{3,2,1,0:T(2,128)(2,1)} %bitcast.99) | data formatting | bytes 12582912
  18.5 1.3 fusion.31
  20.9 0.9 fusion.44
  23.3 25.4 %all-gather.7.cloned.1.call-done = bf16[512,1024]{1,0:T(8,128)(2,1)} async-done(((bf16[64,1024]{1,0:T(8,128)(2,1)}), bf16[512,1024]{1,0:T(8,128)(2,1)}) %all-gather.7.cloned.1.call-update) | async-done | bytes 1048592 | tf_op jit(solution)/shard_map/all_gather | solution.py:169
  48.8 1.7 collective-permute-start
  50.6 12.8 %copy.29 = bf16[3072,3,512]{0,2,1:T(8,128)(2,1)} copy(bf16[3072,3,512]{2,0,1:T(8,128)(2,1)} %param.22) | data formatting | bytes 18874368 | tf_op args[7]
  63.4 5.7 %fusion.47 = f32[256,1536]{1,0:T(8,128)S(1)} fusion(bf16[256,3072]{1,0:T(8,128)(2,1)} %fusion.8, bf16[3072,1536]{0,1:T(8,128)(2,1)} %bitcast.95), kind=kOutput, calls=%fused_computation.99 | convolution fusion | flops 2415919104 | bytes 12582912 | tf_op jit(solution)/shard_map/dot_general | solution.py:150
  69.1 1.2 copy-done.5
  70.3 1.1 slice_multiply_fusion.6
  71.3 2.0 mul.306
  73.4 1.4 reduce_sum.119
  74.8 2.0 mul.315
  76.8 1.4 reduce_sum.120
  78.3 9.5 %collective-permute-done = bf16[256,3072]{1,0:T(8,128)(2,1)} collective-permute-done((bf16[256,3072]{1,0:T(8,128)(2,1)}, bf16[256,3072]{1,0:T(8,128)(2,1)}, u32[]{:S(2)}, u32[]{:S(2)}) %collective-permute-start) | collective-permute-done | bytes 1572896 | tf_op jit(solution)/shard_map/ppermute | solution.py:149
  87.7 5.7 %fusion.48 = f32[256,1536]{1,0:T(8,128)S(1)} fusion(bf16[256,3072]{1,0:T(8,128)(2,1)} %collective-permute-done, bf16[3072,1536]{0,1:T(8,128)(2,1)} %bitcast.96), kind=kOutput, calls=%fused_computation.100 | convolution fusion | flops 2415919104 | bytes 12582912 | tf_op jit(solution)/shard_map/dot_general | solution.py:150
  93.4 1.1 copy-done.7
  94.6 1.1 slice_multiply_fusion.4
  95.6 2.0 mul.331
  97.7 1.4 reduce_sum.122
  99.1 2.0 mul.325
  101.1 2.0 reduce_sum.121
  103.1 1.1 add_rsqrt_fusion.5
  105.6 1.3 fusion.28
  106.9 37.8 %collective-permute-done.1 = bf16[256,3072]{1,0:T(8,128)(2,1)} collective-permute-done((bf16[256,3072]{1,0:T(8,128)(2,1)}, bf16[256,3072]{1,0:T(8,128)(2,1)}, u32[]{:S(2)}, u32[]{:S(2)}) %collective-permute-start.1) | collective-permute-done | bytes 1572896 | tf_op jit(solution)/shard_map/ppermute | solution.py:149
  144.7 38.7 %collective-permute-done.2 = bf16[256,3072]{1,0:T(8,128)(2,1)} collective-permute-done((bf16[256,3072]{1,0:T(8,128)(2,1)}, bf16[256,3072]{1,0:T(8,128)(2,1)}, u32[]{:S(2)}, u32[]{:S(2)}) %collective-permute-start.2) | collective-permute-done | bytes 1572896 | tf_op jit(solution)/shard_map/ppermute | solution.py:149
  183.5 8.5 %collective-permute-done.4 = bf16[64,3072]{1,0:T(8,128)(2,1)} collective-permute-done((bf16[64,3072]{1,0:T(8,128)(2,1)S(1)}, bf16[64,3072]{1,0:T(8,128)(2,1)}, u32[]{:S(2)}, u32[]{:S(2)}) %collective-permute-start.4) | collective-permute-done | bytes 393248 | tf_op jit(solution)/shard_map/ppermute | solution.py:159
  192.1 1.4 collective-permute-start.6
  193.5 7.8 %collective-permute-done.6 = bf16[64,3072]{1,0:T(8,128)(2,1)} collective-permute-done((bf16[64,3072]{1,0:T(8,128)(2,1)}, bf16[64,3072]{1,0:T(8,128)(2,1)}, u32[]{:S(2)}, u32[]{:S(2)}) %collective-permute-start.6) | collective-permute-done | bytes 393248 | tf_op jit(solution)/shard_map/ppermute | solution.py:159
  201.4 3.6 collective-permute-start.8
  204.9 5.6 %collective-permute-done.8 = bf16[64,3072]{1,0:T(8,128)(2,1)} collective-permute-done((bf16[64,3072]{1,0:T(8,128)(2,1)}, bf16[64,3072]{1,0:T(8,128)(2,1)}, u32[]{:S(2)}, u32[]{:S(2)}) %collective-permute-start.8) | collective-permute-done | bytes 393248 | tf_op jit(solution)/shard_map/ppermute | solution.py:159
  210.9 1.0 broadcast.194.clone
  212.0 1.8 fusion.37
  213.8 1.0 broadcast.194.clone.1
  214.8 1.7 constant_dynamic-update-slice_fusion.1
  216.5 1.8 fusion.38
  218.2 1.1 fusion.45
  219.3 5.8 %fusion.49 = f32[256,1536]{1,0:T(8,128)S(1)} fusion(bf16[256,3072]{1,0:T(8,128)(2,1)} %collective-permute-done.1, bf16[3072,1536]{0,1:T(8,128)(2,1)} %bitcast.97), kind=kOutput, calls=%fused_computation.101 | convolution fusion | flops 2415919104 | bytes 12582912 | tf_op jit(solution)/shard_map/dot_general | solution.py:150
  225.1 1.1 copy-done.4
  227.1 2.0 mul.366
  229.1 1.4 reduce_sum.128
  230.9 2.3 slice_multiply_fusion.3
  233.2 2.0 mul.338
  235.3 1.4 reduce_sum.123
  237.8 2.1 fusion.39
  239.9 5.7 %fusion.50 = f32[256,1536]{1,0:T(8,128)S(1)} fusion(bf16[256,3072]{1,0:T(8,128)(2,1)} %collective-permute-done.2, bf16[3072,1536]{0,1:T(8,128)(2,1)} %bitcast.98), kind=kOutput, calls=%fused_computation.102 | convolution fusion | flops 2415919104 | bytes 12582912 | tf_op jit(solution)/shard_map/dot_general | solution.py:150
  245.7 1.1 copy-done.3
  247.6 2.0 mul.372
  249.7 1.4 reduce_sum.129
  251.4 2.3 slice_multiply_fusion.2
  253.8 2.0 mul.345
  255.8 1.4 reduce_sum.124
  257.2 2.0 pad_maximum_fusion.refs_1_
  259.5 2.1 fusion.40
  261.6 57.4 %attend.3 = bf16[768,512]{1,0:T(8,128)(2,1)} custom-call(s32[1]{0:T(128)} %bitcast.refs_0_, bf16[768,512]{1,0:T(8,128)(2,1)} %pad_maximum_fusion.refs_1_, bf16[1024,512]{1,0:T(8,128)(2,1)} %get-tuple-element.26.refs_2_, bf16[1024,512]{1,0:T(8,128)(2,1)} %get-tuple-element.25.refs_3_, bf16[512,512]{1,0:T(8,128)(2,1)} %get-tuple-element.42.refs_4_, ...), custom_call_target="tpu_custom_call" | custom-call | flops 13690208256 | bytes 19398656 | tf_op jit(solution)/shard_map/attend/pallas_call | solution.py:94
  319.0 2.0 fusion.46
  321.1 4.4 %collective-permute-start.3 = (bf16[256,512]{1,0:T(8,128)(2,1)}, bf16[256,512]{1,0:T(8,128)(2,1)}, u32[]{:S(2)}, u32[]{:S(2)}) collective-permute-start(bf16[256,512]{1,0:T(8,128)(2,1)} %get-tuple-element.45), channel_id=1, source_target_pairs={{0,3},{1,0},{2,1},{3,2},{4,7},{5,4},{6,5},{7,6},{8,11},{9,8},{10,9... | collective-permute-start | bytes 786440 | tf_op jit(solution)/shard_map/ppermute | solution.py:187
  326.1 26.1 %attend.2 = bf16[256,512]{1,0:T(8,128)(2,1)} custom-call(s32[1]{0:T(128)} %bitcast.refs_0_, bf16[256,512]{1,0:T(8,128)(2,1)} %get-tuple-element.15.refs_1_, bf16[1024,512]{1,0:T(8,128)(2,1)} %get-tuple-element.26.refs_2_, bf16[1024,512]{1,0:T(8,128)(2,1)} %get-tuple-element.25.refs_3_, bf16[512,512]{1,0:T(8,128)(2,1)} %get-tuple-element.42.refs_4_, ...), custom_call_target="tpu_custom_call" | custom-call | flops 4563402752 | bytes 18350080 | tf_op jit(solution)/shard_map/attend/pallas_call | solution.py:94
  352.2 3.0 fusion.51
  355.2 2.7 convolution_add_fusion.1
  357.9 4.6 %fusion.52 = f32[256,3072]{1,0:T(8,128)} fusion(bf16[256,512]{1,0:T(8,128)(2,1)} %collective-permute-done.7, bf16[512,3072]{1,0:T(8,128)(2,1)} %all-gather.17.cloned.1.call-done), kind=kOutput, calls=%fused_computation.104 | convolution fusion | flops 805306368 | bytes 6553600 | tf_op jit(solution)/shard_map/dot_general | solution.py:191
  362.5 6.5 %fusion.2 = bf16[256,3072]{1,0:T(8,128)(2,1)} fusion(f32[256,3072]{1,0:T(8,128)} %fusion.52, f32[256,3072]{1,0:T(8,128)} %convolution_add_fusion.1, bf16[256,512]{1,0:T(8,128)(2,1)} %collective-permute-done.5, bf16[512,3072]{1,0:T(8,128)(2,1)} %all-gather.15.cloned.1.call-done, bf16[256,3072]{1,0:T(8,128)(2,1)} %param.15, f32[3072]{0:T(1024)S(1)} %copy-done.14), kind=kOutput, calls=%fused_computation.7 | convolution fusion | flops 810024960 | bytes 12857344 | tf_op jit(solution)/shard_map/dot_general | solution.py:191
  (99 shorter events, 9.4 us)
Async XLA Ops:
  7.2 137.5 %copy-start = (bf16[512,3072]{1,0:T(8,128)(2,1)S(1)}, bf16[512,3072]{1,0:T(8,128)(2,1)}, u32[]{:S(2)}) copy-start(bf16[512,3072]{1,0:T(8,128)(2,1)} %param.27) | copy-start | bytes 9437188
  7.2 4.0 %copy-start.13 = (f32[3072]{0:T(1024)S(1)}, f32[3072]{0:T(1024)}, u32[]{:S(2)}) copy-start(f32[3072]{0:T(1024)} %param.17) | copy-start | bytes 36868
  7.2 6.0 %copy-start.2 = (bf16[64,3072]{1,0:T(8,128)(2,1)S(1)}, bf16[64,3072]{1,0:T(8,128)(2,1)}, u32[]{:S(2)}) copy-start(bf16[64,3072]{1,0:T(8,128)(2,1)} %param.16) | copy-start | bytes 1179652
  7.2 41.6 %all-gather.7.cloned.1.call-start = ((), (), s32[]{:S(2)}) async-start(), calls=%async_computation | async-start | bytes 1179648 | tf_op jit(solution)/shard_map/all_gather | solution.py:169
  7.2 3.9 %copy-start.15 = (f32[3072]{0:T(1024)S(1)}, f32[3072]{0:T(1024)}, u32[]{:S(2)}) copy-start(f32[3072]{0:T(1024)} %param.18) | copy-start | bytes 36868
  7.3 4.0 %copy-start.1 = (bf16[256,3072]{1,0:T(8,128)(2,1)S(1)}, bf16[256,3072]{1,0:T(8,128)(2,1)}, u32[]{:S(2)}) copy-start(bf16[256,3072]{1,0:T(8,128)(2,1)} %param.15) | copy-start | bytes 4718596
  13.6 4.9 %copy-start.16 = (f32[3072]{0:T(1024)S(1)}, f32[3072]{0:T(1024)}, u32[]{:S(2)}) copy-start(f32[3072]{0:T(1024)} %param.21) | copy-start | bytes 36868
  13.6 4.9 %copy-start.17 = (f32[3072]{0:T(1024)S(1)}, f32[3072]{0:T(1024)}, u32[]{:S(2)}) copy-start(f32[3072]{0:T(1024)} %param.20) | copy-start | bytes 36868
  18.5 2.2 copy-start.18
  19.8 0.7 copy-start.9
  22.5 239.1 %all-gather.9.cloned.1.call-start = ((), (), s32[]{:S(2)}) async-start(), calls=%async_computation.1 | async-start | bytes 9437184 | tf_op jit(solution)/shard_map/all_gather | solution.py:136
  23.3 238.4 %all-gather.11.cloned.1.call-start = ((), (), s32[]{:S(2)}) async-start(), calls=%async_computation.2 | async-start | bytes 9437184 | tf_op jit(solution)/shard_map/all_gather | solution.py:171
  48.8 303.3 %all-gather.13.cloned.1.call-start = ((), (), s32[]{:S(2)}) async-start(), calls=%async_computation.3 | async-start | bytes 3538944 | tf_op jit(solution)/shard_map/all_gather | solution.py:172
  48.8 38.9 %collective-permute-start = (bf16[256,3072]{1,0:T(8,128)(2,1)}, bf16[256,3072]{1,0:T(8,128)(2,1)}, u32[]{:S(2)}, u32[]{:S(2)}) collective-permute-start(bf16[256,3072]{1,0:T(8,128)(2,1)} %fusion.8), channel_id=1, source_target_pairs={{0,1},{1,2},{2,3},{3,0},{4,5},{5,6},{6,7},{7,4},{8,9},{9,10},{10,1... | collective-permute-start | bytes 4718600 | tf_op jit(solution)/shard_map/ppermute | solution.py:149
  69.1 1.2 copy-start.5
  70.3 7.9 %copy-start.19 = (f32[128]{0:T(128)S(1)}, f32[128]{0:T(128)}, u32[]{:S(2)}) copy-start(f32[128]{0:T(128)} %param.25) | copy-start | bytes 1540
  70.3 7.9 %copy-start.20 = (f32[128]{0:T(128)S(1)}, f32[128]{0:T(128)}, u32[]{:S(2)}) copy-start(f32[128]{0:T(128)} %param.24) | copy-start | bytes 1540
  93.4 1.1 copy-start.7
  103.1 2.5 copy-start.6
  103.1 2.5 copy-start.8
  106.9 37.8 %collective-permute-start.1 = (bf16[256,3072]{1,0:T(8,128)(2,1)}, bf16[256,3072]{1,0:T(8,128)(2,1)}, u32[]{:S(2)}, u32[]{:S(2)}) collective-permute-start(bf16[256,3072]{1,0:T(8,128)(2,1)} %collective-permute-done), channel_id=1, source_target_pairs={{0,1},{1,2},{2,3},{3,0},{4,5},{5,6},{6,7},{7,4},{8,9},{9,10},{10,1... | collective-permute-start | bytes 4718600 | tf_op jit(solution)/shard_map/ppermute | solution.py:149
  144.7 38.8 %collective-permute-start.2 = (bf16[256,3072]{1,0:T(8,128)(2,1)}, bf16[256,3072]{1,0:T(8,128)(2,1)}, u32[]{:S(2)}, u32[]{:S(2)}) collective-permute-start(bf16[256,3072]{1,0:T(8,128)(2,1)} %collective-permute-done.1), channel_id=1, source_target_pairs={{0,1},{1,2},{2,3},{3,0},{4,5},{5,6},{6,7},{7,4},{8,9},{9,10},{10,1... | collective-permute-start | bytes 4718600 | tf_op jit(solution)/shard_map/ppermute | solution.py:149
  183.5 8.5 %collective-permute-start.4 = (bf16[64,3072]{1,0:T(8,128)(2,1)S(1)}, bf16[64,3072]{1,0:T(8,128)(2,1)}, u32[]{:S(2)}, u32[]{:S(2)}) collective-permute-start(bf16[64,3072]{1,0:T(8,128)(2,1)S(1)} %constant_dynamic-slice_fusion), channel_id=1, source_target_pairs={{0,3},{1,0},{2,1},{3,2},{4,7},{5,4},{6,5},{7,6},{8,11},{9,8},{10,9... | collective-permute-start | bytes 1179656 | tf_op jit(solution)/shard_map/ppermute | solution.py:159
  192.0 165.8 %all-gather.17.cloned.1.call-start = ((), (), s32[]{:S(2)}) async-start(), calls=%async_computation.5 | async-start | bytes 3538944 | tf_op jit(solution)/shard_map/all_gather | solution.py:172
  192.1 9.3 %collective-permute-start.6 = (bf16[64,3072]{1,0:T(8,128)(2,1)}, bf16[64,3072]{1,0:T(8,128)(2,1)}, u32[]{:S(2)}, u32[]{:S(2)}) collective-permute-start(bf16[64,3072]{1,0:T(8,128)(2,1)} %collective-permute-done.4), channel_id=1, source_target_pairs={{0,3},{1,0},{2,1},{3,2},{4,7},{5,4},{6,5},{7,6},{8,11},{9,8},{10,9... | collective-permute-start | bytes 1179656 | tf_op jit(solution)/shard_map/ppermute | solution.py:159
  201.4 9.2 %collective-permute-start.8 = (bf16[64,3072]{1,0:T(8,128)(2,1)}, bf16[64,3072]{1,0:T(8,128)(2,1)}, u32[]{:S(2)}, u32[]{:S(2)}) collective-permute-start(bf16[64,3072]{1,0:T(8,128)(2,1)} %collective-permute-done.6), channel_id=1, source_target_pairs={{0,3},{1,0},{2,1},{3,2},{4,7},{5,4},{6,5},{7,6},{8,11},{9,8},{10,9... | collective-permute-start | bytes 1179656 | tf_op jit(solution)/shard_map/ppermute | solution.py:159
  210.6 151.9 %all-gather.15.cloned.1.call-start = ((), (), s32[]{:S(2)}) async-start(), calls=%async_computation.4 | async-start | bytes 3538944 | tf_op jit(solution)/shard_map/all_gather | solution.py:172
  210.9 7.3 %copy-start.11 = (bf16[512,1024]{1,0:T(8,128)(2,1)S(1)}, bf16[512,1024]{1,0:T(8,128)(2,1)}, u32[]{:S(2)}) copy-start(bf16[512,1024]{1,0:T(8,128)(2,1)} %all-gather.7.cloned.1.call-done) | copy-start | bytes 3145732
  225.1 1.1 copy-start.4
  245.6 1.1 copy-start.3
  247.6 9.5 %copy-start.12 = (bf16[256,512]{1,0:T(8,128)(2,1)S(1)}, bf16[256,512]{1,0:T(8,128)(2,1)}, u32[]{:S(2)}) copy-start(bf16[256,512]{1,0:T(8,128)(2,1)} %get-tuple-element.23) | copy-start | bytes 786436
  321.1 31.1 %collective-permute-start.3 = (bf16[256,512]{1,0:T(8,128)(2,1)}, bf16[256,512]{1,0:T(8,128)(2,1)}, u32[]{:S(2)}, u32[]{:S(2)}) collective-permute-start(bf16[256,512]{1,0:T(8,128)(2,1)} %get-tuple-element.45), channel_id=1, source_target_pairs={{0,3},{1,0},{2,1},{3,2},{4,7},{5,4},{6,5},{7,6},{8,11},{9,8},{10,9... | collective-permute-start | bytes 786440 | tf_op jit(solution)/shard_map/ppermute | solution.py:187
  325.5 32.4 %collective-permute-start.7 = (bf16[256,512]{1,0:T(8,128)(2,1)}, bf16[256,512]{1,0:T(8,128)(2,1)}, u32[]{:S(2)}, u32[]{:S(2)}) collective-permute-start(bf16[256,512]{1,0:T(8,128)(2,1)} %get-tuple-element.44), channel_id=1, source_target_pairs={{0,1},{1,2},{2,3},{3,0},{4,5},{5,6},{6,7},{7,4},{8,9},{9,10},{10,1... | collective-permute-start | bytes 786440 | tf_op jit(solution)/shard_map/ppermute | solution.py:187
  325.5 37.0 %collective-permute-start.5 = (bf16[256,512]{1,0:T(8,128)(2,1)}, bf16[256,512]{1,0:T(8,128)(2,1)}, u32[]{:S(2)}, u32[]{:S(2)}) collective-permute-start(bf16[256,512]{1,0:T(8,128)(2,1)} %get-tuple-element.43), channel_id=1, source_target_pairs={{0,2},{1,3},{2,0},{3,1},{4,6},{5,7},{6,4},{7,5},{8,10},{9,11},{10,... | collective-permute-start | bytes 786440 | tf_op jit(solution)/shard_map/ppermute | solution.py:187
  352.1 3.0 copy-start.10
  357.9 4.6 %copy-start.14 = (f32[3072]{0:T(1024)S(1)}, f32[3072]{0:T(1024)}, u32[]{:S(2)}) copy-start(f32[3072]{0:T(1024)} %param.19) | copy-start | bytes 36868
Sparse Core Ops, SparseCore 0:
  22.6 26.0 all-gather.6
  50.7 54.2 all-gather.8
  106.8 54.2 all-gather.10
  192.2 30.2 all-gather.12
  224.2 32.1 all-gather.16
  258.1 32.2 all-gather.14
